TPU v7x, 256 devices: a whole 4x4x8 slice. The times are simulated.
256 devices in a mesh: grow: 16 (over y_lo, x, core), gcol: 16 (over z, y_hi).
Axes of the slice: x: 4, y: 4 (y_hi: 2, y_lo: 2; y = y_hi * 2 + y_lo), z: 8, core: 2. Of those that a mesh axis runs over, the one named last changes fastest.
Arguments:
- eps_static: float32 [12288, 12288], P('grow', 'gcol'), may hold values from -1.8 to 1.8
- eps_imag: float32 [12288, 12288], P('grow', 'gcol'), may hold values from -1.8 to 1.8
- frequency_grid: float32 [3], replicated, may hold values from 0.1 to 2
- band_energy: float32 [32], replicated, may hold values from -2 to 2
- pair_elements: bfloat16 [32, 64, 12288], P('grow', None, 'gcol'), may hold values from -0.0546875 to 0.0546875
Outputs:
- sigma: float32 [3, 64], P(None, 'gcol')
All inputs are finite; a program needn't handle non-finite values.
Results may differ from a plain program's by a relative error of at most 0.0019.
Values may be sent and summed in bfloat16 or wider, within the bound.
A program may use at most 64 MiB of HBM per device.

v0:
```python
import jax
import jax.numpy as jnp
from jax import lax
from jax.sharding import Mesh
from jax.sharding import PartitionSpec as P

NE = 3
GROW = ("grow_0", "grow_1", "grow_2")
GCOL = ("gcol_0", "gcol_1")


def gathered_by_axis(shard, axes, dim):
    for axis in reversed(axes):
        shard = lax.all_gather(shard, axis, axis=dim, tiled=True)
    return shard


def split_up(shard, dim, devices):
    lengths = shard.shape
    parts = shard.reshape(*lengths[:dim], devices, lengths[dim] // devices, *lengths[dim + 1 :])
    return jnp.moveaxis(parts, dim, 0)


def joined_along(parts, dim):
    lengths = list(parts.shape[1:])
    lengths[dim] *= parts.shape[0]
    return jnp.moveaxis(parts, 0, dim).reshape(lengths)


def turned_blocks(parts, axes, order):
    inside = parts.shape[1:]
    out = parts.reshape(*(lax.axis_size(a) for a in axes), *inside)
    for k in order:
        out = lax.all_to_all(out, axes[k], k, k, tiled=True)
    return out.reshape(-1, *inside)


def core_and_chips(shard, groups, order, split_dim, concat_dim):
    devices = lax.axis_size(groups[0]) * lax.axis_size(groups[1])
    parts = split_up(shard, split_dim, devices)
    return joined_along(turned_blocks(parts, groups, order), concat_dim)


def summed_on_arrival(shard, axis, dim):
    devices = lax.axis_size(axis)
    parts = lax.all_to_all(split_up(shard, dim, devices), axis, 0, 0, tiled=True)
    return jnp.sum(parts, axis=0)


def from_everyone(shard, axis):
    copies = jnp.broadcast_to(shard, (lax.axis_size(axis), *shard.shape))
    return lax.all_to_all(copies, axis, split_axis=0, concat_axis=0, tiled=True)


def of_everyone(shard, axis):
    everything = from_everyone(shard, axis)
    return jnp.sum(everything, axis=0)


def shards(eps_static, eps_imag, frequency_grid, band_energy, pair_elements):
    row_count = lax.axis_size(GROW)
    row_index = lax.axis_index(GROW)
    col_index = lax.axis_index(GCOL)
    height = eps_static.shape[0]
    breadth = eps_static.shape[1]
    bands = pair_elements.shape[0] * row_count
    states = pair_elements.shape[1]
    column_panel = lax.all_gather(pair_elements, GROW, axis=0, tiled=True)
    own_bands = gathered_by_axis(pair_elements, GCOL, 2)
    row_panel = core_and_chips(own_bands, (("grow_0", "grow_1"), "grow_2"), (1, 0), 2, 0)
    global_rows = row_index * height + lax.iota(jnp.int32, height)
    global_cols = col_index * breadth + lax.iota(jnp.int32, breadth)
    kronecker = (global_rows[:, None] == global_cols[None, :]).astype(jnp.float32)
    static_part = eps_static - kronecker
    imag_part = eps_imag - kronecker
    spread = static_part - imag_part
    pole_square = (imag_part * imag_part + 0.25) / (spread * spread + 0.25)
    pole_freq = jnp.sqrt(pole_square)
    strength = -static_part * pole_square
    left_rows = row_panel.reshape(bands * states, height)
    right_rows = column_panel.reshape(bands * states, breadth)
    terms = []
    for point in range(NE):
        kernel = (strength / (pole_freq * (pole_freq + frequency_grid[point]))).astype(jnp.bfloat16)
        projected = jnp.dot(left_rows, kernel, preferred_element_type=jnp.float32)
        terms.append(jnp.sum(projected * right_rows, axis=1))
    quad = jnp.stack(terms).reshape(NE, bands, states)
    offset_energy = frequency_grid[:, None] - band_energy[None, :]
    weight = 1.0 / (1.0 + offset_energy * offset_energy)
    partial_sigma = jnp.einsum("em,ems->es", weight, quad)
    shares = summed_on_arrival(partial_sigma, GCOL, 1)
    return of_everyone(shares, GROW)


def solution(mesh):
    finer = Mesh(
        mesh.devices.reshape(2, 4, 2, 8, 2), ("grow_0", "grow_1", "grow_2", "gcol_0", "gcol_1")
    )
    in_specs = (P(GROW, GCOL), P(GROW, GCOL), P(), P(), P(GROW, None, GCOL))
    out_specs = P(None, GCOL)
    return jax.shard_map(
        shards, mesh=finer, in_specs=in_specs, out_specs=out_specs, check_vma=False
    )
```

profile of v0, /device:TPU:1, one launch (start us, length us, event | category | flops | bytes accessed | tf_op | source)
XLA Modules:
  0.0 211.0 jit_solution(8430354224616254626)
XLA Ops:
  6.5 10.5 %all_gather.9 = bf16[2,64,1536]{2,1,0:T(8,128)(2,1)} all-gather(bf16[2,64,768]{2,1,0:T(8,128)(2,1)} %param.9), channel_id=1, replica_groups=mesh['grow_0'=2,'grow_1'=4,'grow_2'=2,'gcol_0'=8,'gcol_1'=2] {'gcol_1'}, dimensions={2}, use_global_device_ids=true | all-gather | bytes 589824 | tf_op jit(solution)/shard_map/all_gather | solution.py:14
  17.1 0.7 all-gather.5.cloned.1.call-update
  17.8 46.2 %all-gather.3.cloned.1.call-done = bf16[2,64,12288]{2,1,0:T(8,128)(2,1)} async-done(((bf16[2,64,1536]{2,1,0:T(8,128)(2,1)}), bf16[2,64,12288]{2,1,0:T(8,128)(2,1)}) %all-gather.3.cloned.1.call-update) | async-done | bytes 3145744 | tf_op jit(solution)/shard_map/all_gather | solution.py:14
  64.0 2.7 %copy.47 = bf16[16,8,16,768]{3,2,1,0:T(8,128)(2,1)S(1)} copy(bf16[16,8,16,768]{3,1,2,0:T(8,128)(2,1)} %bitcast.42) | data formatting | bytes 6291456
  66.7 0.2 bitcast_bitcast_fusion
  66.9 1.0 copy.36
  67.9 0.3 copy.37
  68.3 7.1 %all_to_all.20 = bf16[8,2,2,64,768]{4,3,2,0,1:T(8,128)(2,1)S(1)} all-to-all(bf16[8,2,2,64,768]{4,3,2,0,1:T(8,128)(2,1)S(1)} %copy.37), channel_id=1, replica_groups=mesh['grow_0'=2,'grow_1'=4,'grow_2'=2,'gcol_0'=8,'gcol_1'=2] {'grow_2'}, dimensions={1} | all-to-all | bytes 6291456 | tf_op jit(solution)/shard_map/all_to_all | solution.py:34
  75.4 2.0 copy.38
  77.4 5.0 %all-to-all-start.1 = ((bf16[8,2,2,64,768]{4,3,2,1,0:T(8,128)(2,1)}), bf16[8,2,2,64,768]{4,3,2,1,0:T(8,128)(2,1)S(1)}, u32[]{:S(2)}, u32[]{:S(2)}) async-start(bf16[8,2,2,64,768]{4,3,2,1,0:T(8,128)(2,1)} %copy.38), calls=%async_computation.1 | async-start | bytes 6291456 | tf_op jit(solution)/shard_map/all_to_all | solution.py:34
  82.4 0.7 fusion.26
  83.2 53.7 %all-gather.5.cloned.1.call-done = bf16[32,64,768]{2,1,0:T(8,128)(2,1)} async-done(((bf16[2,64,768]{2,1,0:T(8,128)(2,1)}), bf16[32,64,768]{2,1,0:T(8,128)(2,1)}) %all-gather.5.cloned.1.call-update) | async-done | bytes 3145744 | tf_op jit(solution)/shard_map/all_gather | solution.py:68
  136.8 5.0 %bitcast_convert_fusion = f32[2048,768]{1,0:T(8,128)} fusion(bf16[32,64,768]{2,1,0:T(8,128)(2,1)} %all-gather.5.cloned.1.call-done), kind=kLoop, calls=%fused_computation.12 | loop fusion | flops 1572864 | bytes 9437184 | tf_op jit(solution)/shard_map/convert_element_type | solution.py:86
  141.9 6.6 %copy.39 = f32[2048,768]{0,1:T(8,128)} copy(f32[2048,768]{1,0:T(8,128)} %bitcast_convert_fusion) | data formatting | bytes 12582912 | tf_op jit(solution)/shard_map/convert_element_type | solution.py:86
  148.5 9.0 %fusion = bf16[2048]{0:T(1024)(128)(2,1)S(1)} fusion(f32[2048,768]{0,1:T(8,128)} %copy.39, bf16[2048,768]{1,0:T(8,128)(2,1)S(1)} %bitcast.39, f32[]{:T(128)} %bitcast.10, f32[768,768]{1,0:T(8,128)} %param.5, s32[768]{0:T(1024)S(1)} %get-tuple-element.8, s32[768]{0:T(1024)S(1)} %get-tuple-element.9, f32[768,768]{1,0:T(8,128)} %param.6), kind=kOutput, calls=%fused_computation.1 | convolution fusion | flops 2428499968 | bytes 14166020 | tf_op jit(solution)/shard_map/dot_general | solution.py:85
  157.5 0.1 stack.14
  157.6 9.0 %fusion.1 = bf16[2048]{0:T(1024)(128)(2,1)S(1)} fusion(f32[2048,768]{0,1:T(8,128)} %copy.39, bf16[2048,768]{1,0:T(8,128)(2,1)S(1)} %bitcast.40, f32[]{:T(128)} %bitcast.7, f32[768,768]{1,0:T(8,128)} %param.5, s32[768]{0:T(1024)S(1)} %get-tuple-element.8, s32[768]{0:T(1024)S(1)} %get-tuple-element.9, f32[768,768]{1,0:T(8,128)} %param.6), kind=kOutput, calls=%fused_computation.3 | convolution fusion | flops 2428499968 | bytes 14166020 | tf_op jit(solution)/shard_map/dot_general | solution.py:85
  166.6 0.1 stack.13
  166.7 9.0 %fusion.2 = bf16[2048]{0:T(1024)(128)(2,1)S(1)} fusion(f32[2048,768]{0,1:T(8,128)} %copy.39, bf16[2048,768]{1,0:T(8,128)(2,1)S(1)} %bitcast.41, f32[]{:T(128)} %bitcast.1, f32[768,768]{1,0:T(8,128)} %param.5, s32[768]{0:T(1024)S(1)} %get-tuple-element.8, s32[768]{0:T(1024)S(1)} %get-tuple-element.9, f32[768,768]{1,0:T(8,128)} %param.6), kind=kOutput, calls=%fused_computation.5 | convolution fusion | flops 2428499968 | bytes 14166020 | tf_op jit(solution)/shard_map/dot_general | solution.py:85
  175.8 0.1 fusion.18
  175.9 0.1 reshape.31
  176.0 17.6 %all_to_all.21 = f32[16,3,4]{2,1,0:T(4,128)S(1)} all-to-all(f32[16,3,4]{2,1,0:T(4,128)S(1)} %copy.42), channel_id=1, replica_groups=mesh['grow_0'=2,'grow_1'=4,'grow_2'=2,'gcol_0'=8,'gcol_1'=2] {'gcol_0','..., dimensions={0} | all-to-all | bytes 1536 | tf_op jit(solution)/shard_map/all_to_all | solution.py:46
  193.6 9.9 %all_to_all.22 = f32[16,3,4]{2,1,0:T(4,128)S(1)} all-to-all(f32[16,3,4]{2,1,0:T(4,128)S(1)} %broadcast_in_dim.2), channel_id=1, replica_groups=mesh['grow_0'=2,'grow_1'=4,'grow_2'=2,'gcol_0'=8,'gcol_1'=2] {'grow_0','..., dimensions={0} | all-to-all | bytes 1536 | tf_op jit(solution)/shard_map/all_to_all | solution.py:52
  203.5 0.6 reduce_sum.49
  (15 shorter events, 0.3 us)
Async XLA Ops:
  6.5 57.5 %all-gather.3.cloned.1.call-start = ((), (), s32[]{:S(2)}) async-start(), calls=%async_computation.4 | async-start | bytes 3538944 | tf_op jit(solution)/shard_map/all_gather | solution.py:14
  17.0 119.8 %all-gather.5.cloned.1.call-start = ((), (), s32[]{:S(2)}) async-start(), calls=%async_computation.5 | async-start | bytes 3342336 | tf_op jit(solution)/shard_map/all_gather | solution.py:68
  77.4 5.0 %copy-start = (f32[3]{0:T(128)S(1)}, f32[3]{0:T(128)}, u32[]{:S(2)}) copy-start(f32[3]{0:T(128)} %param.7) | copy-start | bytes 40
  77.4 5.7 %copy-start.1 = (f32[32]{0:T(128)S(1)}, f32[32]{0:T(128)}, u32[]{:S(2)}) copy-start(f32[32]{0:T(128)} %param.8) | copy-start | bytes 388
  77.4 71.1 %all-to-all-start.1 = ((bf16[8,2,2,64,768]{4,3,2,1,0:T(8,128)(2,1)}), bf16[8,2,2,64,768]{4,3,2,1,0:T(8,128)(2,1)S(1)}, u32[]{:S(2)}, u32[]{:S(2)}) async-start(bf16[8,2,2,64,768]{4,3,2,1,0:T(8,128)(2,1)} %copy.38), calls=%async_computation.1 | async-start | bytes 6291456 | tf_op jit(solution)/shard_map/all_to_all | solution.py:34
Sparse Core Ops, SparseCore 0:
  17.2 46.8 all-gather.2
  65.9 70.9 all-gather.4
where the time goes:
time: 211 us
  waiting for transfers between devices  101 us (48%)
  blocking collectives  45.1 us (21%)
  matrix products  27.1 us (13%)
  local copies, waits for them, and re-layouts  13.8 us (7%)
  between operations  13.5 us (6%)
  other arithmetic  5.74 us (3%)
  starting transfers between devices  5.07 us (2%)
    all_gather x1, waiting for transfers between devices, shards(): column_panel = lax.all_gather(pair_elements, GROW, axis=0, tiled=True)  53.7 us
    all_gather x1, waiting for transfers between devices, gathered_by_axis(): shard = lax.all_gather(shard, axis, axis=dim, tiled=True)  46.2 us
    dot_general x3, matrix products, shards(): projected = jnp.dot(left_rows, kernel, preferred_element_type=jnp.float32)  27 us
    all_to_all x1, blocking collectives, summed_on_arrival(): lax.all_to_all(split_up(shard, dim, devices), axis, 0, 0, tiled=True)  17.6 us
    all_gather x1, blocking collectives, gathered_by_axis(): shard = lax.all_gather(shard, axis, axis=dim, tiled=True)  10.5 us
    all_to_all x1, blocking collectives, from_everyone(): return lax.all_to_all(copies, axis, split_axis=0, concat_axis=0, tiled=True)  9.92 us
    all_to_all x1, blocking collectives, turned_blocks(): out = lax.all_to_all(out, axes[k], k, k, tiled=True)  7.13 us
    convert_element_type x1, local copies, waits for them, and re-layouts, shards(): terms.append(jnp.sum(projected * right_rows, axis=1))  6.6 us
  transfers between devices with their start and end apart: 3, of which 2 were waited for; matrix products, arithmetic and copies ran while one was open for 9% of the time, Pallas kernels for 0%

commit v1 on v0

--- a/solution.py
+++ b/solution.py
@@ -3,6 +3,7 @@
 from jax import lax
 from jax.sharding import Mesh
 from jax.sharding import PartitionSpec as P
+from jax.lax import all_to_all, psum
 
 NE = 3
 GROW = ("grow_0", "grow_1", "grow_2")
@@ -65,7 +66,9 @@
     breadth = eps_static.shape[1]
     bands = pair_elements.shape[0] * row_count
     states = pair_elements.shape[1]
-    column_panel = lax.all_gather(pair_elements, GROW, axis=0, tiled=True)
+    answer = tuple((pair_elements for _ in range(psum(1, GROW))))
+    w_next = jnp.stack(answer, axis=0)
+    column_panel = jnp.concatenate(all_to_all(w_next, GROW, 0, 0), axis=0)
     own_bands = gathered_by_axis(pair_elements, GCOL, 2)
     row_panel = core_and_chips(own_bands, (("grow_0", "grow_1"), "grow_2"), (1, 0), 2, 0)
     global_rows = row_index * height + lax.iota(jnp.int32, height)

time: 211 us -> 237 us (1.12)
  waiting for transfers between devices: 101 us -> 113 us
  blocking collectives: 45.1 us -> 52.5 us
  starting transfers between devices: 5.07 us -> 9.21 us
    all_gather x1 -> x0, waiting for transfers between devices: 53.7 us -> none  [shards(): column_panel = lax.all_gather(pair_elements, GROW, axis=0, tiled=True)]
    all_to_all x0 -> x1, waiting for transfers between devices: none -> 40 us  [shards(): column_panel = jnp.concatenate(all_to_all(w_next, GROW, 0, 0), axis=0)]
    all_to_all x1, waiting for transfers between devices: 0.01 us -> 25.9 us  [turned_blocks(): out = lax.all_to_all(out, axes[k], k, k, tiled=True)]
    all_to_all x1, blocking collectives: 9.92 us -> 19.4 us  [from_everyone(): return lax.all_to_all(copies, axis, split_axis=0, concat_axis=0, tiled=True)]
    all_to_all x0 -> x1, starting transfers between devices: none -> 5.56 us  [shards(): column_panel = jnp.concatenate(all_to_all(w_next, GROW, 0, 0), axis=0)]
  transfers between devices with their start and end apart: 3 -> 3, of which waited for: 2 -> 3; matrix products, arithmetic and copies ran while one was open for 9% -> 6% of each run, Pallas kernels for 0% -> 0%
where the time goes in v1:
time: 237 us
  waiting for transfers between devices  113 us (48%)
  blocking collectives  52.5 us (22%)
  matrix products  27.1 us (11%)
  local copies, waits for them, and re-layouts  15.8 us (7%)
  between operations  13.5 us (6%)
  starting transfers between devices  9.21 us (4%)
  other arithmetic  5.74 us (2%)
    all_gather x1, waiting for transfers between devices, gathered_by_axis(): shard = lax.all_gather(shard, axis, axis=dim, tiled=True)  47 us
    all_to_all x1, waiting for transfers between devices, shards(): column_panel = jnp.concatenate(all_to_all(w_next, GROW, 0, 0), axis=0)  40 us
    dot_general x3, matrix products, shards(): projected = jnp.dot(left_rows, kernel, preferred_element_type=jnp.float32)  27 us
    all_to_all x1, waiting for transfers between devices, turned_blocks(): out = lax.all_to_all(out, axes[k], k, k, tiled=True)  25.9 us
    all_to_all x1, blocking collectives, from_everyone(): return lax.all_to_all(copies, axis, split_axis=0, concat_axis=0, tiled=True)  19.4 us
    all_to_all x1, blocking collectives, summed_on_arrival(): lax.all_to_all(split_up(shard, dim, devices), axis, 0, 0, tiled=True)  15.2 us
    all_gather x1, blocking collectives, gathered_by_axis(): shard = lax.all_gather(shard, axis, axis=dim, tiled=True)  10.5 us
    all_to_all x1, blocking collectives, turned_blocks(): out = lax.all_to_all(out, axes[k], k, k, tiled=True)  7.26 us
  transfers between devices with their start and end apart: 3, of which 3 were waited for; matrix products, arithmetic and copies ran while one was open for 6% of the time, Pallas kernels for 0%

profile of v1, /device:TPU:1, one launch (start us, length us, event | category | flops | bytes accessed | tf_op | source)
XLA Modules:
  0.0 236.7 jit_solution(14691951150774784493)
XLA Ops:
  6.5 10.5 %all_gather.6 = bf16[2,64,1536]{2,1,0:T(8,128)(2,1)} all-gather(bf16[2,64,768]{2,1,0:T(8,128)(2,1)} %param.9), channel_id=1, replica_groups=mesh['grow_0'=2,'grow_1'=4,'grow_2'=2,'gcol_0'=8,'gcol_1'=2] {'gcol_1'}, dimensions={2}, use_global_device_ids=true | all-gather | bytes 589824 | tf_op jit(solution)/shard_map/all_gather | solution.py:15
  17.1 47.0 %all-gather.2.cloned.1.call-done = bf16[2,64,12288]{2,1,0:T(8,128)(2,1)} async-done(((bf16[2,64,1536]{2,1,0:T(8,128)(2,1)}), bf16[2,64,12288]{2,1,0:T(8,128)(2,1)}) %all-gather.2.cloned.1.call-update) | async-done | bytes 3145744 | tf_op jit(solution)/shard_map/all_gather | solution.py:15
  64.0 2.7 %copy.47 = bf16[16,8,16,768]{3,2,1,0:T(8,128)(2,1)S(1)} copy(bf16[16,8,16,768]{3,1,2,0:T(8,128)(2,1)} %bitcast.42) | data formatting | bytes 6291456
  66.7 0.2 bitcast_bitcast_fusion
  66.9 1.0 copy.36
  67.9 0.3 copy.37
  68.3 7.3 %all_to_all.25 = bf16[8,2,2,64,768]{4,3,2,0,1:T(8,128)(2,1)S(1)} all-to-all(bf16[8,2,2,64,768]{4,3,2,0,1:T(8,128)(2,1)S(1)} %copy.37), channel_id=1, replica_groups=mesh['grow_0'=2,'grow_1'=4,'grow_2'=2,'gcol_0'=8,'gcol_1'=2] {'grow_2'}, dimensions={1} | all-to-all | bytes 6291456 | tf_op jit(solution)/shard_map/all_to_all | solution.py:35
  75.5 2.1 stack.10
  77.6 5.6 %all-to-all-start.2 = ((bf16[16,2,64,768]{3,2,1,0:T(8,128)(2,1)}), bf16[16,2,64,768]{3,2,1,0:T(8,128)(2,1)}, u32[]{:S(2)}, u32[]{:S(2)}) async-start(bf16[16,2,64,768]{3,2,1,0:T(8,128)(2,1)} %stack.10), calls=%async_computation.2 | async-start | bytes 6291456 | tf_op jit(solution)/shard_map/all_to_all | solution.py:71
  83.2 1.9 copy.38
  85.1 40.0 %all-to-all-done.2 = bf16[16,2,64,768]{3,2,1,0:T(8,128)(2,1)} async-done(((bf16[16,2,64,768]{3,2,1,0:T(8,128)(2,1)}), bf16[16,2,64,768]{3,2,1,0:T(8,128)(2,1)}, u32[]{:S(2)}, u32[]{:S(2)}) %all-to-all-start.2) | async-done | bytes 3145760 | tf_op jit(solution)/shard_map/all_to_all | solution.py:71
  125.0 3.6 %all-to-all-start.1 = ((bf16[8,2,2,64,768]{4,3,2,1,0:T(8,128)(2,1)}), bf16[8,2,2,64,768]{4,3,2,1,0:T(8,128)(2,1)S(1)}, u32[]{:S(2)}, u32[]{:S(2)}) async-start(bf16[8,2,2,64,768]{4,3,2,1,0:T(8,128)(2,1)} %copy.38), calls=%async_computation.1 | async-start | bytes 6291456 | tf_op jit(solution)/shard_map/all_to_all | solution.py:35
  128.7 0.7 fusion.26
  129.4 5.0 %bitcast_convert_fusion = f32[2048,768]{1,0:T(8,128)} fusion(bf16[16,2,64,768]{3,2,1,0:T(8,128)(2,1)} %all-to-all-done.2), kind=kLoop, calls=%fused_computation.12 | loop fusion | flops 1572864 | bytes 9437184 | tf_op jit(solution)/shard_map/convert_element_type | solution.py:89
  134.5 6.6 %copy.39 = f32[2048,768]{0,1:T(8,128)} copy(f32[2048,768]{1,0:T(8,128)} %bitcast_convert_fusion) | data formatting | bytes 12582912 | tf_op jit(solution)/shard_map/convert_element_type | solution.py:89
  141.1 25.9 %all-to-all-done.1 = bf16[8,2,2,64,768]{4,3,2,1,0:T(8,128)(2,1)S(1)} async-done(((bf16[8,2,2,64,768]{4,3,2,1,0:T(8,128)(2,1)}), bf16[8,2,2,64,768]{4,3,2,1,0:T(8,128)(2,1)S(1)}, u32[]{:S(2)}, u32[]{:S(2)}) %all-to-all-start.1) | async-done | bytes 3145760 | tf_op jit(solution)/shard_map/all_to_all | solution.py:35
  167.0 9.0 %fusion = bf16[2048]{0:T(1024)(128)(2,1)S(1)} fusion(f32[2048,768]{0,1:T(8,128)} %copy.39, bf16[2048,768]{1,0:T(8,128)(2,1)S(1)} %bitcast.39, f32[]{:T(128)} %bitcast.10, f32[768,768]{1,0:T(8,128)} %param.5, s32[768]{0:T(1024)S(1)} %get-tuple-element.8, s32[768]{0:T(1024)S(1)} %get-tuple-element.9, f32[768,768]{1,0:T(8,128)} %param.6), kind=kOutput, calls=%fused_computation.1 | convolution fusion | flops 2428499968 | bytes 14166020 | tf_op jit(solution)/shard_map/dot_general | solution.py:88
  176.1 9.0 %fusion.1 = bf16[2048]{0:T(1024)(128)(2,1)S(1)} fusion(f32[2048,768]{0,1:T(8,128)} %copy.39, bf16[2048,768]{1,0:T(8,128)(2,1)S(1)} %bitcast.40, f32[]{:T(128)} %bitcast.7, f32[768,768]{1,0:T(8,128)} %param.5, s32[768]{0:T(1024)S(1)} %get-tuple-element.8, s32[768]{0:T(1024)S(1)} %get-tuple-element.9, f32[768,768]{1,0:T(8,128)} %param.6), kind=kOutput, calls=%fused_computation.3 | convolution fusion | flops 2428499968 | bytes 14166020 | tf_op jit(solution)/shard_map/dot_general | solution.py:88
  185.1 9.0 %fusion.2 = bf16[2048]{0:T(1024)(128)(2,1)S(1)} fusion(f32[2048,768]{0,1:T(8,128)} %copy.39, bf16[2048,768]{1,0:T(8,128)(2,1)S(1)} %bitcast.41, f32[]{:T(128)} %bitcast.1, f32[768,768]{1,0:T(8,128)} %param.5, s32[768]{0:T(1024)S(1)} %get-tuple-element.8, s32[768]{0:T(1024)S(1)} %get-tuple-element.9, f32[768,768]{1,0:T(8,128)} %param.6), kind=kOutput, calls=%fused_computation.5 | convolution fusion | flops 2428499968 | bytes 14166020 | tf_op jit(solution)/shard_map/dot_general | solution.py:88
  194.2 0.1 fusion.18
  194.4 0.1 reshape.32
  194.5 15.2 %all_to_all.26 = f32[16,3,4]{2,1,0:T(4,128)S(1)} all-to-all(f32[16,3,4]{2,1,0:T(4,128)S(1)} %copy.42), channel_id=1, replica_groups=mesh['grow_0'=2,'grow_1'=4,'grow_2'=2,'gcol_0'=8,'gcol_1'=2] {'gcol_0','..., dimensions={0} | all-to-all | bytes 1536 | tf_op jit(solution)/shard_map/all_to_all | solution.py:47
  209.8 19.4 %all_to_all.27 = f32[16,3,4]{2,1,0:T(4,128)S(1)} all-to-all(f32[16,3,4]{2,1,0:T(4,128)S(1)} %broadcast_in_dim.2), channel_id=1, replica_groups=mesh['grow_0'=2,'grow_1'=4,'grow_2'=2,'gcol_0'=8,'gcol_1'=2] {'grow_0','..., dimensions={0} | all-to-all | bytes 1536 | tf_op jit(solution)/shard_map/all_to_all | solution.py:53
  229.2 0.6 reduce_sum.49
  (17 shorter events, 0.4 us)
Async XLA Ops:
  6.5 57.5 %all-gather.2.cloned.1.call-start = ((), (), s32[]{:S(2)}) async-start(), calls=%async_computation.5 | async-start | bytes 3538944 | tf_op jit(solution)/shard_map/all_gather | solution.py:15
  68.3 7.3 %copy-start = (bf16[2,64,768]{2,1,0:T(8,128)(2,1)S(1)}, bf16[2,64,768]{2,1,0:T(8,128)(2,1)}, u32[]{:S(2)}) copy-start(bf16[2,64,768]{2,1,0:T(8,128)(2,1)} %param.9) | copy-start | bytes 589828
  77.6 47.4 %all-to-all-start.2 = ((bf16[16,2,64,768]{3,2,1,0:T(8,128)(2,1)}), bf16[16,2,64,768]{3,2,1,0:T(8,128)(2,1)}, u32[]{:S(2)}, u32[]{:S(2)}) async-start(bf16[16,2,64,768]{3,2,1,0:T(8,128)(2,1)} %stack.10), calls=%async_computation.2 | async-start | bytes 6291456 | tf_op jit(solution)/shard_map/all_to_all | solution.py:71
  85.1 43.7 %copy-start.1 = (f32[3]{0:T(128)S(1)}, f32[3]{0:T(128)}, u32[]{:S(2)}) copy-start(f32[3]{0:T(128)} %param.7) | copy-start | bytes 40
  85.1 44.3 %copy-start.2 = (f32[32]{0:T(128)S(1)}, f32[32]{0:T(128)}, u32[]{:S(2)}) copy-start(f32[32]{0:T(128)} %param.8) | copy-start | bytes 388
  125.0 41.9 %all-to-all-start.1 = ((bf16[8,2,2,64,768]{4,3,2,1,0:T(8,128)(2,1)}), bf16[8,2,2,64,768]{4,3,2,1,0:T(8,128)(2,1)S(1)}, u32[]{:S(2)}, u32[]{:S(2)}) async-start(bf16[8,2,2,64,768]{4,3,2,1,0:T(8,128)(2,1)} %copy.38), calls=%async_computation.1 | async-start | bytes 6291456 | tf_op jit(solution)/shard_map/all_to_all | solution.py:35
Sparse Core Ops, SparseCore 0:
  17.2 46.8 all-gather.1
